TPU v7x, 32 devices: a whole 2x2x4 slice. The times are simulated.
32 devices in a mesh: rep: 4 (over z), tp: 8 (over y, x, core).
Axes of the slice: x: 2, y: 2, z: 4, core: 2. Of those that a mesh axis runs over, the one named last changes fastest.
Arguments:
- exp_hidden: bfloat16 [256, 8192], P('rep', 'tp'), may hold values from -160 to 160
- exp_pre_gain: float32 [8192], P('tp'), may hold values from 0.25 to 1.75
- exp_gate: bfloat16 [8192, 28672], P('tp', 'rep'), may hold values from -0.0625 to 0.0625
- exp_up: bfloat16 [8192, 28672], P('tp', 'rep'), may hold values from -0.0625 to 0.0625
- exp_down: bfloat16 [28672, 8192], P('rep', 'tp'), may hold values from -0.03125 to 0.03125
- exp_out_gain: float32 [8192], P('tp'), may hold values from 0.25 to 1.75
- exp_head: bfloat16 [8192, 65536], P(None, ('rep', 'tp')), may hold values from -10 to 10
- ama_hidden: bfloat16 [256, 4096], P('rep', 'tp'), may hold values from -160 to 160
- ama_out_gain: float32 [4096], P('tp'), may hold values from 0.25 to 1.75
- ama_head: bfloat16 [4096, 65536], P(None, ('rep', 'tp')), may hold values from -10 to 10
- logit_scale: float32 [256], replicated, may hold values from 0.25 to 3
- prompt_of: int32 [256], replicated, may hold values from 0 to 7
- prior_picks: int32 [8, 24], replicated, may hold values from 0 to 65535
- valid_mask: int32 [65536], P(('rep', 'tp')), may hold values 0 or 1
Outputs:
- scores: float32 [256, 65536], P(None, ('rep', 'tp'))
- beam_best: float32 [256], replicated
All inputs are finite; a program needn't handle non-finite values. No bound on the sum of `valid_mask` on one device may be relied on, other than what follows from the above.
Results may differ from a plain program's by a relative error of at most 0.0034.
Values may be sent and summed in bfloat16 or wider, within the bound.
No kernel may reach another device: no remote copies, remote signals or barrier semaphores. Data moves between devices by JAX's collectives and lax.ppermute only.
A program may use at most 192 MiB of HBM per device.

v0:
```python
import jax
import jax.numpy as jnp
from jax import lax
from jax.sharding import PartitionSpec as P

DE = 8192
DA = 4096
norm_epsilon = 1e-05
contrast_weight = 0.5
hamming_weight = 0.7


def scaled_rows(values, squares, width, gain):
    return (values * lax.rsqrt(squares[:, None] / width + norm_epsilon) * gain).astype(jnp.bfloat16)


def both_halves(rows_in, gate_weight, up_weight):
    gate = jnp.dot(rows_in, gate_weight, preferred_element_type=jnp.float32)
    up = jnp.dot(rows_in, up_weight, preferred_element_type=jnp.float32)
    return jnp.concatenate([gate, up], axis=1)


def gated_rows(summed, width):
    return (jax.nn.silu(summed[:, :width]) * summed[:, width:]).astype(jnp.bfloat16)


def body(
    exp_hidden,
    exp_pre_gain,
    exp_gate,
    exp_up,
    exp_down,
    exp_out_gain,
    exp_head,
    ama_hidden,
    ama_out_gain,
    ama_head,
    logit_scale,
    prompt_of,
    prior_picks,
    valid_mask,
):
    values_exp = exp_hidden.astype(jnp.float32)
    values_ama = ama_hidden.astype(jnp.float32)
    squares_exp = lax.psum(jnp.sum(values_exp * values_exp, axis=1), "tp")
    normed_exp = scaled_rows(values_exp, squares_exp, DE, exp_pre_gain)
    rows_exp = lax.all_gather(normed_exp, "rep", axis=0, tiled=True)
    width_exp = exp_gate.shape[1]
    summed_exp = lax.psum_scatter(
        both_halves(rows_exp, exp_gate, exp_up), "tp", scatter_dimension=0, tiled=True
    )
    hidden_exp = gated_rows(summed_exp, width_exp)
    term_exp = jnp.dot(
        lax.all_gather(hidden_exp, "tp", axis=0, tiled=True),
        exp_down,
        preferred_element_type=jnp.float32,
    )
    out_exp = lax.psum_scatter(term_exp, "rep", scatter_dimension=0, tiled=True)
    layer_exp = values_exp + out_exp
    final_sq_exp, final_sq_ama = lax.psum(
        (jnp.sum(layer_exp * layer_exp, axis=1), jnp.sum(values_ama * values_ama, axis=1)), "tp"
    )
    final_exp = scaled_rows(layer_exp, final_sq_exp, DE, exp_out_gain)
    final_ama = scaled_rows(values_ama, final_sq_ama, DA, ama_out_gain)
    features_exp, features_ama = (
        lax.all_gather(final_exp, "tp", axis=1, tiled=True),
        lax.all_gather(final_ama, "tp", axis=1, tiled=True),
    )
    full_exp, full_ama = (
        lax.all_gather(features_exp, "rep", axis=0, tiled=True),
        lax.all_gather(features_ama, "rep", axis=0, tiled=True),
    )
    logits_exp = logit_scale[:, None] * jnp.dot(
        full_exp, exp_head, preferred_element_type=jnp.float32
    )
    logits_ama = logit_scale[:, None] * jnp.dot(
        full_ama, ama_head, preferred_element_type=jnp.float32
    )
    top_exp, top_ama = lax.pmax(
        (jnp.max(logits_exp, axis=1), jnp.max(logits_ama, axis=1)), ("rep", "tp")
    )
    local_exp = jnp.sum(jnp.exp(logits_exp - top_exp[:, None]), axis=1)
    local_ama = jnp.sum(jnp.exp(logits_ama - top_ama[:, None]), axis=1)
    total_exp, total_ama = lax.psum((local_exp, local_ama), ("rep", "tp"))
    logp_exp = logits_exp - top_exp[:, None] - jnp.log(total_exp)[:, None]
    logp_ama = logits_ama - top_ama[:, None] - jnp.log(total_ama)[:, None]
    entries = exp_head.shape[1]
    first_entry = lax.axis_index(("rep", "tp")) * entries
    vocab_ids = first_entry + jnp.arange(entries, dtype=jnp.int32)
    picks_row = jnp.take(prior_picks, prompt_of, axis=0)
    counts = jnp.sum(
        (picks_row[:, :, None] == vocab_ids[None, None, :]).astype(jnp.float32), axis=1
    )
    valid = valid_mask.astype(jnp.float32)[None, :]
    scores = logp_exp - contrast_weight * valid * logp_ama - hamming_weight * counts
    beam_best = lax.pmax(jnp.max(scores, axis=1), ("rep", "tp"))
    return (scores, beam_best)


def solution(mesh):
    placed = (
        P("rep", "tp"),
        P("tp"),
        P("tp", "rep"),
        P("tp", "rep"),
        P("rep", "tp"),
        P("tp"),
        P(None, ("rep", "tp")),
        P("rep", "tp"),
        P("tp"),
        P(None, ("rep", "tp")),
        P(),
        P(),
        P(),
        P(("rep", "tp")),
    )
    return jax.shard_map(
        body, mesh=mesh, in_specs=placed, out_specs=(P(None, ("rep", "tp")), P()), check_vma=False
    )
```

profile of v0, /device:TPU:0, one launch (start us, length us, event | category | flops | bytes accessed | tf_op | source)
XLA Modules:
  0.0 552.7 jit_solution(7237676692740054795)
XLA Ops:
  7.2 1.0 fusion.1
  8.3 15.2 %psum.35 = f32[64]{0:T(128)S(1)} all-reduce(f32[64]{0:T(128)S(1)} %fusion.1), channel_id=1, replica_groups=mesh['rep'=4,'tp'=8] {'tp'}, use_global_device_ids=true, to_apply=%region_1.0 | all-reduce | flops 64 | bytes 512 | tf_op jit(solution)/shard_map/psum | solution.py:45
  23.4 1.0 fusion.3
  24.4 15.9 %all_gather.18 = bf16[256,1024]{1,0:T(8,128)(2,1)S(1)} all-gather(bf16[64,1024]{1,0:T(8,128)(2,1)S(1)} %fusion.3), channel_id=1, replica_groups=mesh['rep'=4,'tp'=8] {'rep'}, dimensions={0}, use_global_device_ids=true | all-gather | bytes 655360 | tf_op jit(solution)/shard_map/all_gather | solution.py:47
  40.4 7.4 %fusion.10 = f32[256,7168]{1,0:T(8,128)S(1)} fusion(bf16[256,1024]{1,0:T(8,128)(2,1)S(1)} %all_gather.18, bf16[1024,7168]{1,0:T(8,128)(2,1)} %param.16), kind=kOutput, calls=%fused_computation.35 | convolution fusion | flops 3758096384 | bytes 22544384 | tf_op jit(solution)/shard_map/dot_general | solution.py:18
  47.8 1.9 copy-done.2
  49.7 4.1 fusion.11
  53.8 5.5 pad_maximum_fusion
  59.3 103.7 %reduce-scatter.3.cloned.1.call-done = f32[32,14336]{1,0:T(8,128)} async-done(((f32[256,14336]{1,0:T(8,128)}), f32[32,14336]{1,0:T(8,128)}) %reduce-scatter.3.cloned.1.call-update) | async-done | bytes 1835024 | tf_op jit(solution)/shard_map/reduce_scatter | solution.py:49
  163.1 2.5 fusion
  165.7 34.4 %all-gather.5.cloned.1.call-done = bf16[256,7168]{1,0:T(8,128)(2,1)} async-done(((bf16[32,7168]{1,0:T(8,128)(2,1)}), bf16[256,7168]{1,0:T(8,128)(2,1)}) %all-gather.5.cloned.1.call-update) | async-done | bytes 3670032 | tf_op jit(solution)/shard_map/all_gather | solution.py:54
  200.1 11.2 %fusion.12 = f32[256,1024]{1,0:T(8,128)} fusion(bf16[256,7168]{1,0:T(8,128)(2,1)} %all-gather.5.cloned.1.call-done, bf16[7168,1024]{1,0:T(8,128)(2,1)} %param.18), kind=kOutput, calls=%fused_computation.37 | convolution fusion | flops 3758096384 | bytes 19398656 | tf_op jit(solution)/shard_map/dot_general | solution.py:53
  211.4 0.1 fusion.4
  211.5 27.3 %reduce-scatter.5.cloned.1.call-done = f32[64,1024]{1,0:T(8,128)} async-done(((f32[256,1024]{1,0:T(8,128)}), f32[64,1024]{1,0:T(8,128)}) %reduce-scatter.5.cloned.1.call-update) | async-done | bytes 262160 | tf_op jit(solution)/shard_map/reduce_scatter | solution.py:58
  238.8 1.1 multiply_reduce_fusion
  239.9 13.2 %all-reduce.2 = (f32[64]{0:T(128)S(1)}, f32[64]{0:T(128)S(1)}) all-reduce(f32[64]{0:T(128)S(1)} %fusion.4, f32[64]{0:T(128)S(1)} %multiply_reduce_fusion), channel_id=1, replica_groups=mesh['rep'=4,'tp'=8] {'tp'}, use_global_device_ids=true, to_apply=%region_11.12 | all-reduce | flops 128 | bytes 1024 | tf_op jit(solution)/shard_map/psum | solution.py:60
  253.1 1.7 multiply_convert_fusion
  255.0 10.5 %all_gather.22 = bf16[64,4096]{1,0:T(8,128)(2,1)} all-gather(bf16[64,512]{1,0:T(8,128)(2,1)S(1)} %fusion.6), channel_id=1, replica_groups=mesh['rep'=4,'tp'=8] {'tp'}, dimensions={1}, use_global_device_ids=true | all-gather | bytes 589824 | tf_op jit(solution)/shard_map/all_gather | solution.py:67
  265.6 0.2 all-gather.9.cloned.1.call-start
  265.8 9.6 %all-gather.7.cloned.1.call-done = bf16[64,8192]{1,0:T(8,128)(2,1)} async-done(((bf16[64,1024]{1,0:T(8,128)(2,1)}), bf16[64,8192]{1,0:T(8,128)(2,1)}) %all-gather.7.cloned.1.call-update) | async-done | bytes 1048592 | tf_op jit(solution)/shard_map/all_gather | solution.py:66
  275.5 0.7 gather_fusion
  276.3 0.1 broadcast_select_fusion
  276.4 20.6 %convert_reduce_fusion = f32[256,2048]{1,0:T(8,128)} fusion(s32[2048]{0:T(1024)S(1)} %iota_add_fusion, s32[256,24]{1,0:T(8,128)S(1)} %broadcast_select_fusion), kind=kLoop, calls=%fused_computation.1 | loop fusion | flops 37224448 | bytes 2129920 | tf_op jit(solution)/shard_map/reduce_sum | solution.py:91
  297.0 25.5 %all-gather.11.cloned.1.call-done = bf16[256,4096]{1,0:T(8,128)(2,1)} async-done(((bf16[64,4096]{1,0:T(8,128)(2,1)}), bf16[256,4096]{1,0:T(8,128)(2,1)}) %all-gather.11.cloned.1.call-update) | async-done | bytes 2097168 | tf_op jit(solution)/shard_map/all_gather | solution.py:71
  322.5 8.8 %fusion.8 = (f32[256]{0:T(256)S(1)}, f32[256,2048]{1,0:T(8,128)S(1)}) fusion(bf16[256,4096]{1,0:T(8,128)(2,1)} %all-gather.11.cloned.1.call-done, bf16[4096,2048]{1,0:T(8,128)(2,1)} %param.23, f32[256]{0:T(256)S(1)} %copy-done.9), kind=kOutput, calls=%fused_computation.33 | convolution fusion | flops 4296015872 | bytes 20973568 | tf_op jit(solution)/shard_map/dot_general | solution.py:76
  331.3 72.2 %all-gather.9.cloned.1.call-done = bf16[256,8192]{1,0:T(8,128)(2,1)} async-done(((bf16[64,8192]{1,0:T(8,128)(2,1)}), bf16[256,8192]{1,0:T(8,128)(2,1)}) %all-gather.9.cloned.1.call-update) | async-done | bytes 4194320 | tf_op jit(solution)/shard_map/all_gather | solution.py:70
  403.5 17.2 %fusion.9 = (f32[256]{0:T(256)S(1)}, f32[256,2048]{1,0:T(8,128)}) fusion(bf16[256,8192]{1,0:T(8,128)(2,1)} %all-gather.9.cloned.1.call-done, bf16[8192,2048]{1,0:T(8,128)(2,1)} %param.20, f32[256]{0:T(256)S(1)} %copy-done.9), kind=kOutput, calls=%fused_computation.34 | convolution fusion | flops 8590983168 | bytes 39847936 | tf_op jit(solution)/shard_map/dot_general | solution.py:73
  420.7 38.6 %all-reduce.1 = (f32[256]{0:T(256)S(1)}, f32[256]{0:T(256)S(1)}) all-reduce(f32[256]{0:T(256)S(1)} %get-tuple-element.10, f32[256]{0:T(256)S(1)} %get-tuple-element.12), channel_id=1, replica_groups=mesh['rep'=4,'tp'=8] {'rep','tp'}, use_global_device_ids=true, to_apply=%region_13.14 | all-reduce | flops 512 | bytes 4096 | tf_op jit(solution)/shard_map/pmax | solution.py:79
  459.4 2.3 exponential_reduce_fusion
  461.7 40.4 %all-reduce = (f32[256]{0:T(256)S(1)}, f32[256]{0:T(256)S(1)}) all-reduce(f32[256]{0:T(256)S(1)} %get-tuple-element.14, f32[256]{0:T(256)S(1)} %get-tuple-element.15), channel_id=1, replica_groups=mesh['rep'=4,'tp'=8] {'rep','tp'}, use_global_device_ids=true, to_apply=%region_15.16 | all-reduce | flops 512 | bytes 4096 | tf_op jit(solution)/shard_map/psum | solution.py:84
  502.1 4.4 fusion.7
  506.5 39.4 %pmax.23 = f32[256]{0:T(256)} all-reduce(f32[256]{0:T(256)S(1)} %get-tuple-element.8), channel_id=1, replica_groups=mesh['rep'=4,'tp'=8] {'rep','tp'}, use_global_device_ids=true, to_apply=%region_18.19 | all-reduce | flops 256 | bytes 2048 | tf_op jit(solution)/shard_map/pmax | solution.py:96
  (41 shorter events, 0.5 us)
Async XLA Ops:
  7.2 268.3 %copy-start = (s32[8,24]{1,0:T(8,128)S(1)}, s32[8,24]{1,0:T(8,128)}, u32[]{:S(2)}) copy-start(s32[8,24]{1,0:T(8,128)} %param.26) | copy-start | bytes 2308
  7.2 155.9 %reduce-scatter.3.cloned.1.call-start = ((), (), s32[]{:S(2)}) async-start(), calls=%async_computation.2 | async-start | bytes 16515072 | tf_op jit(solution)/shard_map/reduce_scatter | solution.py:49
  40.4 9.3 %copy-start.2 = (bf16[1024,7168]{1,0:T(8,128)(2,1)S(1)}, bf16[1024,7168]{1,0:T(8,128)(2,1)}, u32[]{:S(2)}) copy-start(bf16[1024,7168]{1,0:T(8,128)(2,1)} %param.17) | copy-start | bytes 44040196
  59.3 140.8 %all-gather.5.cloned.1.call-start = ((), (), s32[]{:S(2)}) async-start(), calls=%async_computation.3 | async-start | bytes 4128768 | tf_op jit(solution)/shard_map/all_gather | solution.py:54
  165.6 45.8 %copy-start.4 = (bf16[64,512]{1,0:T(8,128)(2,1)S(1)}, bf16[64,512]{1,0:T(8,128)(2,1)}, u32[]{:S(2)}) copy-start(bf16[64,512]{1,0:T(8,128)(2,1)} %param.21) | copy-start | bytes 196612
  165.6 73.2 %copy-start.3 = (bf16[64,1024]{1,0:T(8,128)(2,1)S(1)}, bf16[64,1024]{1,0:T(8,128)(2,1)}, u32[]{:S(2)}) copy-start(bf16[64,1024]{1,0:T(8,128)(2,1)} %param.14) | copy-start | bytes 393220
  165.6 87.5 %copy-start.6 = (f32[1024]{0:T(1024)S(1)}, f32[1024]{0:T(1024)}, u32[]{:S(2)}) copy-start(f32[1024]{0:T(1024)} %param.19) | copy-start | bytes 12292
  165.6 89.3 %copy-start.7 = (f32[512]{0:T(512)S(1)}, f32[512]{0:T(512)}, u32[]{:S(2)}) copy-start(f32[512]{0:T(512)} %param.22) | copy-start | bytes 6148
  165.6 73.2 %reduce-scatter.5.cloned.1.call-start = ((), (), s32[]{:S(2)}) async-start(), calls=%async_computation.4 | async-start | bytes 1310720 | tf_op jit(solution)/shard_map/reduce_scatter | solution.py:58
  211.3 64.1 %copy-start.8 = (s32[256]{0:T(256)S(1)}, s32[256]{0:T(256)}, u32[]{:S(2)}) copy-start(s32[256]{0:T(256)} %param.25) | copy-start | bytes 3076
  211.3 64.9 %copy-start.5 = (s32[2048]{0:T(1024)S(1)}, s32[2048]{0:T(1024)}, u32[]{:S(2)}) copy-start(s32[2048]{0:T(1024)} %param.27) | copy-start | bytes 24580
  211.4 111.2 %copy-start.9 = (f32[256]{0:T(256)S(1)}, f32[256]{0:T(256)}, u32[]{:S(2)}) copy-start(f32[256]{0:T(256)} %param.24) | copy-start | bytes 3076
  211.4 64.0 %all-gather.7.cloned.1.call-start = ((), (), s32[]{:S(2)}) async-start(), calls=%async_computation.5 | async-start | bytes 1179648 | tf_op jit(solution)/shard_map/all_gather | solution.py:66
  254.8 67.7 %all-gather.11.cloned.1.call-start = ((), (), s32[]{:S(2)}) async-start(), calls=%async_computation.7 | async-start | bytes 2621440 | tf_op jit(solution)/shard_map/all_gather | solution.py:71
  265.6 138.0 %all-gather.9.cloned.1.call-start = ((), (), s32[]{:S(2)}) async-start(), calls=%async_computation.6 | async-start | bytes 5242880 | tf_op jit(solution)/shard_map/all_gather | solution.py:70
  502.1 43.8 %copy-start.1 = (s32[8,24]{1,0:T(8,128)S(1)}, s32[8,24]{1,0:T(8,128)}, u32[]{:S(2)}) copy-start(s32[8,24]{1,0:T(8,128)} %param.26) | copy-start | bytes 2308
Sparse Core Ops, SparseCore 0:
  59.4 103.6 reduce-scatter.2
  165.7 34.3 all-gather.4
  211.5 27.2 reduce-scatter.4
  255.0 20.3 all-gather.6
  276.8 45.6 all-gather.10
  323.9 79.5 all-gather.8
where the time goes:
time: 553 us
  waiting for transfers between devices  273 us (49%)
  blocking collectives  173 us (31%)
  matrix products  48.7 us (9%)
  other arithmetic  40.4 us (7%)
  between operations  14.3 us (3%)
    reduce_scatter x1, waiting for transfers between devices, body(): lax.psum_scatter(both_halves(rows_exp, exp_gate, exp_up), 'tp', scatter_d...  104 us
    all_gather x1, waiting for transfers between devices, body(): lax.all_gather(features_exp, 'rep', axis=0, tiled=True)  72.2 us
    psum x1, blocking collectives, body(): total_exp, total_ama = lax.psum((local_exp, local_ama), ('rep', 'tp'))  40.4 us
    pmax x1, blocking collectives, body(): beam_best = lax.pmax(jnp.max(scores, axis=1), ('rep', 'tp'))  39.4 us
    pmax x1, blocking collectives, body(): lax.pmax((jnp.max(logits_exp, axis=1), jnp.max(logits_ama, axis=1)), ('re...  38.6 us
    all_gather x1, waiting for transfers between devices, body(): lax.all_gather(hidden_exp, 'tp', axis=0, tiled=True)  34.4 us
    reduce_scatter x1, waiting for transfers between devices, body(): out_exp = lax.psum_scatter(term_exp, 'rep', scatter_dimension=0, tiled=True)  27.3 us
    all_gather x1, waiting for transfers between devices, body(): lax.all_gather(features_ama, 'rep', axis=0, tiled=True)  25.5 us
  transfers between devices with their start and end apart: 6, of which 6 were waited for; matrix products, arithmetic and copies ran while one was open for 6% of the time, Pallas kernels for 0%

commit v1 on v0

--- a/solution.py
+++ b/solution.py
@@ -1,3 +1,4 @@
+import functools
 import jax
 import jax.numpy as jnp
 from jax import lax
@@ -8,6 +9,26 @@
 norm_epsilon = 1e-05
 contrast_weight = 0.5
 hamming_weight = 0.7
+
+
+def _save_lines(xin, device_axis):
+    arr_out, shaped, parts_out = (
+        lax.axis_size(device_axis),
+        lax.axis_index(device_axis),
+        xin.shape[0],
+    )
+    panels = list(map(lambda at: (at, (at + 1) % arr_out), range(arr_out)))
+    formed = xin
+    row_out = jnp.zeros((*xin.shape[:0], arr_out * parts_out, *xin.shape[1:]), xin.dtype)
+    for rr in tuple(range(arr_out)):
+        big = (shaped - rr) % arr_out
+        row_out = lax.dynamic_update_slice_in_dim(row_out, formed, big * parts_out, axis=0)
+        if rr < arr_out - 1:
+            formed = lax.ppermute(formed, device_axis, panels)
+    return row_out
+
+
+convert_heaps_now = functools.partial(_save_lines, device_axis="tp")
 
 
 def scaled_rows(values, squares, width, gain):
@@ -50,11 +71,7 @@
         both_halves(rows_exp, exp_gate, exp_up), "tp", scatter_dimension=0, tiled=True
     )
     hidden_exp = gated_rows(summed_exp, width_exp)
-    term_exp = jnp.dot(
-        lax.all_gather(hidden_exp, "tp", axis=0, tiled=True),
-        exp_down,
-        preferred_element_type=jnp.float32,
-    )
+    term_exp = jnp.dot(convert_heaps_now(hidden_exp), exp_down, preferred_element_type=jnp.float32)
     out_exp = lax.psum_scatter(term_exp, "rep", scatter_dimension=0, tiled=True)
     layer_exp = values_exp + out_exp
     final_sq_exp, final_sq_ama = lax.psum(

time: 553 us -> 582 us (1.052)
  waiting for transfers between devices: 273 us -> 295 us
  local copies, waits for them, and re-layouts: 2.73 us -> 10.6 us
    ppermute x0 -> x7, waiting for transfers between devices: none -> 56.7 us  [_save_lines(): formed = lax.ppermute(formed, device_axis, panels)]
    all_gather x1 -> x0, waiting for transfers between devices: 34.4 us -> none  [body(): lax.all_gather(hidden_exp, 'tp', axis=0, tiled=True)]
  transfers between devices with their start and end apart: 6 -> 12, of which waited for: 6 -> 12; matrix products, arithmetic and copies ran while one was open for 6% -> 6% of each run, Pallas kernels for 0% -> 0%
where the time goes in v1:
time: 582 us; the launch traced here: 581 us
  waiting for transfers between devices  295 us (51%)
  blocking collectives  173 us (30%)
  matrix products  48.7 us (8%)
  other arithmetic  39 us (7%)
  between operations  14 us (2%)
  local copies, waits for them, and re-layouts  10.6 us (2%)
    reduce_scatter x1, waiting for transfers between devices, body(): lax.psum_scatter(both_halves(rows_exp, exp_gate, exp_up), 'tp', scatter_d...  104 us
    all_gather x1, waiting for transfers between devices, body(): lax.all_gather(features_exp, 'rep', axis=0, tiled=True)  72.2 us
    ppermute x7, waiting for transfers between devices, _save_lines(): formed = lax.ppermute(formed, device_axis, panels)  56.7 us
    psum x1, blocking collectives, body(): total_exp, total_ama = lax.psum((local_exp, local_ama), ('rep', 'tp'))  40.4 us
    pmax x1, blocking collectives, body(): beam_best = lax.pmax(jnp.max(scores, axis=1), ('rep', 'tp'))  39.4 us
    pmax x1, blocking collectives, body(): lax.pmax((jnp.max(logits_exp, axis=1), jnp.max(logits_ama, axis=1)), ('re...  38.6 us
    reduce_scatter x1, waiting for transfers between devices, body(): out_exp = lax.psum_scatter(term_exp, 'rep', scatter_dimension=0, tiled=True)  27.3 us
    all_gather x1, waiting for transfers between devices, body(): lax.all_gather(features_ama, 'rep', axis=0, tiled=True)  25.5 us
  transfers between devices with their start and end apart: 12, of which 12 were waited for; matrix products, arithmetic and copies ran while one was open for 6% of the time, Pallas kernels for 0%

profile of v1, /device:TPU:0, one launch (start us, length us, event | category | flops | bytes accessed | tf_op | source)
XLA Modules:
  0.0 581.1 jit_solution(13912002577094385289)
XLA Ops:
  8.3 15.2 %psum.35 = f32[64]{0:T(128)S(1)} all-reduce(f32[64]{0:T(128)S(1)} %fusion.1), channel_id=1, replica_groups=mesh['rep'=4,'tp'=8] {'tp'}, use_global_device_ids=true, to_apply=%region_1.0 | all-reduce | flops 64 | bytes 512 | tf_op jit(solution)/shard_map/psum | solution.py:66
  24.4 15.9 %all_gather.15 = bf16[256,1024]{1,0:T(8,128)(2,1)S(1)} all-gather(bf16[64,1024]{1,0:T(8,128)(2,1)S(1)} %fusion.3), channel_id=1, replica_groups=mesh['rep'=4,'tp'=8] {'rep'}, dimensions={0}, use_global_device_ids=true | all-gather | bytes 655360 | tf_op jit(solution)/shard_map/all_gather | solution.py:68
  40.4 7.4 %fusion.11 = f32[256,7168]{1,0:T(8,128)S(1)} fusion(bf16[256,1024]{1,0:T(8,128)(2,1)S(1)} %all_gather.15, bf16[1024,7168]{1,0:T(8,128)(2,1)} %param.16), kind=kOutput, calls=%fused_computation.43 | convolution fusion | flops 3758096384 | bytes 22544384 | tf_op jit(solution)/shard_map/dot_general | solution.py:39
  47.8 1.9 copy-done.2
  49.7 4.1 fusion.12
  53.8 5.5 pad_maximum_fusion
  59.4 103.7 %reduce-scatter.3.cloned.1.call-done = f32[32,14336]{1,0:T(8,128)} async-done(((f32[256,14336]{1,0:T(8,128)}), f32[32,14336]{1,0:T(8,128)}) %reduce-scatter.3.cloned.1.call-update) | async-done | bytes 1835024 | tf_op jit(solution)/shard_map/reduce_scatter | solution.py:70
  163.1 2.2 broadcast_in_dim.11
  166.3 8.8 %collective-permute-done = bf16[32,7168]{1,0:T(8,128)(2,1)S(1)} collective-permute-done((bf16[32,7168]{1,0:T(8,128)(2,1)S(1)}, bf16[32,7168]{1,0:T(8,128)(2,1)S(1)}, u32[]{:S(2)}, u32[]{:S(2)}) %collective-permute-start) | collective-permute-done | bytes 458784 | tf_op jit(solution)/shard_map/ppermute | solution.py:27
  175.9 8.0 %collective-permute-done.1 = bf16[32,7168]{1,0:T(8,128)(2,1)S(1)} collective-permute-done((bf16[32,7168]{1,0:T(8,128)(2,1)S(1)}, bf16[32,7168]{1,0:T(8,128)(2,1)S(1)}, u32[]{:S(2)}, u32[]{:S(2)}) %collective-permute-start.1) | collective-permute-done | bytes 458784 | tf_op jit(solution)/shard_map/ppermute | solution.py:27
  184.8 8.0 %collective-permute-done.2 = bf16[32,7168]{1,0:T(8,128)(2,1)S(1)} collective-permute-done((bf16[32,7168]{1,0:T(8,128)(2,1)S(1)}, bf16[32,7168]{1,0:T(8,128)(2,1)S(1)}, u32[]{:S(2)}, u32[]{:S(2)}) %collective-permute-start.2) | collective-permute-done | bytes 458784 | tf_op jit(solution)/shard_map/ppermute | solution.py:27
  193.5 8.0 %collective-permute-done.3 = bf16[32,7168]{1,0:T(8,128)(2,1)S(1)} collective-permute-done((bf16[32,7168]{1,0:T(8,128)(2,1)S(1)}, bf16[32,7168]{1,0:T(8,128)(2,1)S(1)}, u32[]{:S(2)}, u32[]{:S(2)}) %collective-permute-start.3) | collective-permute-done | bytes 458784 | tf_op jit(solution)/shard_map/ppermute | solution.py:27
  202.3 8.0 %collective-permute-done.4 = bf16[32,7168]{1,0:T(8,128)(2,1)S(1)} collective-permute-done((bf16[32,7168]{1,0:T(8,128)(2,1)S(1)}, bf16[32,7168]{1,0:T(8,128)(2,1)S(1)}, u32[]{:S(2)}, u32[]{:S(2)}) %collective-permute-start.4) | collective-permute-done | bytes 458784 | tf_op jit(solution)/shard_map/ppermute | solution.py:27
  211.2 8.0 %collective-permute-done.5 = bf16[32,7168]{1,0:T(8,128)(2,1)S(1)} collective-permute-done((bf16[32,7168]{1,0:T(8,128)(2,1)S(1)}, bf16[32,7168]{1,0:T(8,128)(2,1)S(1)}, u32[]{:S(2)}, u32[]{:S(2)}) %collective-permute-start.5) | collective-permute-done | bytes 458784 | tf_op jit(solution)/shard_map/ppermute | solution.py:27
  220.0 8.0 %collective-permute-done.6 = bf16[32,7168]{1,0:T(8,128)(2,1)S(1)} collective-permute-done((bf16[32,7168]{1,0:T(8,128)(2,1)S(1)}, bf16[32,7168]{1,0:T(8,128)(2,1)S(1)}, u32[]{:S(2)}, u32[]{:S(2)}) %collective-permute-start.6) | collective-permute-done | bytes 458784 | tf_op jit(solution)/shard_map/ppermute | solution.py:27
  228.8 11.2 %fusion.13 = f32[256,1024]{1,0:T(8,128)} fusion(bf16[256,7168]{1,0:T(8,128)(2,1)} %constant_dynamic-update-slice_fusion, bf16[7168,1024]{1,0:T(8,128)(2,1)} %param.18), kind=kOutput, calls=%fused_computation.45 | convolution fusion | flops 3758096384 | bytes 19398656 | tf_op jit(solution)/shard_map/dot_general | solution.py:74
  240.2 27.3 %reduce-scatter.5.cloned.1.call-done = f32[64,1024]{1,0:T(8,128)} async-done(((f32[256,1024]{1,0:T(8,128)}), f32[64,1024]{1,0:T(8,128)}) %reduce-scatter.5.cloned.1.call-update) | async-done | bytes 262160 | tf_op jit(solution)/shard_map/reduce_scatter | solution.py:75
  267.5 1.1 multiply_reduce_fusion
  268.6 13.2 %all-reduce.2 = (f32[64]{0:T(128)S(1)}, f32[64]{0:T(128)S(1)}) all-reduce(f32[64]{0:T(128)S(1)} %fusion.4, f32[64]{0:T(128)S(1)} %multiply_reduce_fusion), channel_id=1, replica_groups=mesh['rep'=4,'tp'=8] {'tp'}, use_global_device_ids=true, to_apply=%region_11.12 | all-reduce | flops 128 | bytes 1024 | tf_op jit(solution)/shard_map/psum | solution.py:77
  281.8 1.7 multiply_convert_fusion
  283.7 10.5 %all_gather.18 = bf16[64,4096]{1,0:T(8,128)(2,1)} all-gather(bf16[64,512]{1,0:T(8,128)(2,1)S(1)} %fusion.6), channel_id=1, replica_groups=mesh['rep'=4,'tp'=8] {'tp'}, dimensions={1}, use_global_device_ids=true | all-gather | bytes 589824 | tf_op jit(solution)/shard_map/all_gather | solution.py:84
  294.5 9.6 %all-gather.4.cloned.1.call-done = bf16[64,8192]{1,0:T(8,128)(2,1)} async-done(((bf16[64,1024]{1,0:T(8,128)(2,1)}), bf16[64,8192]{1,0:T(8,128)(2,1)}) %all-gather.4.cloned.1.call-update) | async-done | bytes 1048592 | tf_op jit(solution)/shard_map/all_gather | solution.py:83
  305.1 20.6 %convert_reduce_fusion = f32[256,2048]{1,0:T(8,128)} fusion(s32[2048]{0:T(1024)S(1)} %iota_add_fusion, s32[256,24]{1,0:T(8,128)S(1)} %broadcast_select_fusion), kind=kLoop, calls=%fused_computation.1 | loop fusion | flops 37224448 | bytes 2129920 | tf_op jit(solution)/shard_map/reduce_sum | solution.py:108
  325.7 25.5 %all-gather.8.cloned.1.call-done = bf16[256,4096]{1,0:T(8,128)(2,1)} async-done(((bf16[64,4096]{1,0:T(8,128)(2,1)}), bf16[256,4096]{1,0:T(8,128)(2,1)}) %all-gather.8.cloned.1.call-update) | async-done | bytes 2097168 | tf_op jit(solution)/shard_map/all_gather | solution.py:88
  351.2 8.8 %fusion.9 = (f32[256]{0:T(256)S(1)}, f32[256,2048]{1,0:T(8,128)S(1)}) fusion(bf16[256,4096]{1,0:T(8,128)(2,1)} %all-gather.8.cloned.1.call-done, bf16[4096,2048]{1,0:T(8,128)(2,1)} %param.23, f32[256]{0:T(256)S(1)} %copy-done.10), kind=kOutput, calls=%fused_computation.41 | convolution fusion | flops 4296015872 | bytes 20973568 | tf_op jit(solution)/shard_map/dot_general | solution.py:93
  360.0 72.2 %all-gather.6.cloned.1.call-done = bf16[256,8192]{1,0:T(8,128)(2,1)} async-done(((bf16[64,8192]{1,0:T(8,128)(2,1)}), bf16[256,8192]{1,0:T(8,128)(2,1)}) %all-gather.6.cloned.1.call-update) | async-done | bytes 4194320 | tf_op jit(solution)/shard_map/all_gather | solution.py:87
  432.2 17.2 %fusion.10 = (f32[256]{0:T(256)S(1)}, f32[256,2048]{1,0:T(8,128)}) fusion(bf16[256,8192]{1,0:T(8,128)(2,1)} %all-gather.6.cloned.1.call-done, bf16[8192,2048]{1,0:T(8,128)(2,1)} %param.20, f32[256]{0:T(256)S(1)} %copy-done.10), kind=kOutput, calls=%fused_computation.42 | convolution fusion | flops 8590983168 | bytes 39847936 | tf_op jit(solution)/shard_map/dot_general | solution.py:90
  449.4 38.6 %all-reduce.1 = (f32[256]{0:T(256)S(1)}, f32[256]{0:T(256)S(1)}) all-reduce(f32[256]{0:T(256)S(1)} %get-tuple-element.12, f32[256]{0:T(256)S(1)} %get-tuple-element.14), channel_id=1, replica_groups=mesh['rep'=4,'tp'=8] {'rep','tp'}, use_global_device_ids=true, to_apply=%region_13.14 | all-reduce | flops 512 | bytes 4096 | tf_op jit(solution)/shard_map/pmax | solution.py:96
  488.1 2.3 exponential_reduce_fusion
  490.3 40.4 %all-reduce = (f32[256]{0:T(256)S(1)}, f32[256]{0:T(256)S(1)}) all-reduce(f32[256]{0:T(256)S(1)} %get-tuple-element.16, f32[256]{0:T(256)S(1)} %get-tuple-element.17), channel_id=1, replica_groups=mesh['rep'=4,'tp'=8] {'rep','tp'}, use_global_device_ids=true, to_apply=%region_15.16 | all-reduce | flops 512 | bytes 4096 | tf_op jit(solution)/shard_map/psum | solution.py:101
  530.8 4.4 fusion.7
  535.2 39.4 %pmax.23 = f32[256]{0:T(256)} all-reduce(f32[256]{0:T(256)S(1)} %get-tuple-element.8), channel_id=1, replica_groups=mesh['rep'=4,'tp'=8] {'rep','tp'}, use_global_device_ids=true, to_apply=%region_18.19 | all-reduce | flops 256 | bytes 2048 | tf_op jit(solution)/shard_map/pmax | solution.py:113
  (62 shorter events, 10.4 us)
Async XLA Ops:
  7.2 297.0 %copy-start = (s32[8,24]{1,0:T(8,128)S(1)}, s32[8,24]{1,0:T(8,128)}, u32[]{:S(2)}) copy-start(s32[8,24]{1,0:T(8,128)} %param.26) | copy-start | bytes 2308
  7.2 155.9 %reduce-scatter.3.cloned.1.call-start = ((), (), s32[]{:S(2)}) async-start(), calls=%async_computation.2 | async-start | bytes 16515072 | tf_op jit(solution)/shard_map/reduce_scatter | solution.py:70
  40.4 9.3 %copy-start.2 = (bf16[1024,7168]{1,0:T(8,128)(2,1)S(1)}, bf16[1024,7168]{1,0:T(8,128)(2,1)}, u32[]{:S(2)}) copy-start(bf16[1024,7168]{1,0:T(8,128)(2,1)} %param.17) | copy-start | bytes 44040196
  59.3 208.2 %reduce-scatter.5.cloned.1.call-start = ((), (), s32[]{:S(2)}) async-start(), calls=%async_computation.3 | async-start | bytes 1310720 | tf_op jit(solution)/shard_map/reduce_scatter | solution.py:75
  163.1 2.2 copy-start.4
  166.3 8.8 %collective-permute-start = (bf16[32,7168]{1,0:T(8,128)(2,1)S(1)}, bf16[32,7168]{1,0:T(8,128)(2,1)S(1)}, u32[]{:S(2)}, u32[]{:S(2)}) collective-permute-start(bf16[32,7168]{1,0:T(8,128)(2,1)S(1)} %get-tuple-element.11), channel_id=1, source_target_pairs={{0,1},{1,2},{2,3},{3,4},{4,5},{5,6},{6,7},{7,0},{8,9},{9,10},{10,1... | collective-permute-start | bytes 1376264 | tf_op jit(solution)/shard_map/ppermute | solution.py:27
  175.1 8.8 %collective-permute-start.1 = (bf16[32,7168]{1,0:T(8,128)(2,1)S(1)}, bf16[32,7168]{1,0:T(8,128)(2,1)S(1)}, u32[]{:S(2)}, u32[]{:S(2)}) collective-permute-start(bf16[32,7168]{1,0:T(8,128)(2,1)S(1)} %collective-permute-done), channel_id=1, source_target_pairs={{0,1},{1,2},{2,3},{3,4},{4,5},{5,6},{6,7},{7,0},{8,9},{9,10},{10,1... | collective-permute-start | bytes 1376264 | tf_op jit(solution)/shard_map/ppermute | solution.py:27
  183.9 8.8 %collective-permute-start.2 = (bf16[32,7168]{1,0:T(8,128)(2,1)S(1)}, bf16[32,7168]{1,0:T(8,128)(2,1)S(1)}, u32[]{:S(2)}, u32[]{:S(2)}) collective-permute-start(bf16[32,7168]{1,0:T(8,128)(2,1)S(1)} %collective-permute-done.1), channel_id=1, source_target_pairs={{0,1},{1,2},{2,3},{3,4},{4,5},{5,6},{6,7},{7,0},{8,9},{9,10},{10,1... | collective-permute-start | bytes 1376264 | tf_op jit(solution)/shard_map/ppermute | solution.py:27
  192.7 8.8 %collective-permute-start.3 = (bf16[32,7168]{1,0:T(8,128)(2,1)S(1)}, bf16[32,7168]{1,0:T(8,128)(2,1)S(1)}, u32[]{:S(2)}, u32[]{:S(2)}) collective-permute-start(bf16[32,7168]{1,0:T(8,128)(2,1)S(1)} %collective-permute-done.2), channel_id=1, source_target_pairs={{0,1},{1,2},{2,3},{3,4},{4,5},{5,6},{6,7},{7,0},{8,9},{9,10},{10,1... | collective-permute-start | bytes 1376264 | tf_op jit(solution)/shard_map/ppermute | solution.py:27
  201.5 8.8 %collective-permute-start.4 = (bf16[32,7168]{1,0:T(8,128)(2,1)S(1)}, bf16[32,7168]{1,0:T(8,128)(2,1)S(1)}, u32[]{:S(2)}, u32[]{:S(2)}) collective-permute-start(bf16[32,7168]{1,0:T(8,128)(2,1)S(1)} %collective-permute-done.3), channel_id=1, source_target_pairs={{0,1},{1,2},{2,3},{3,4},{4,5},{5,6},{6,7},{7,0},{8,9},{9,10},{10,1... | collective-permute-start | bytes 1376264 | tf_op jit(solution)/shard_map/ppermute | solution.py:27
  210.3 8.8 %collective-permute-start.5 = (bf16[32,7168]{1,0:T(8,128)(2,1)S(1)}, bf16[32,7168]{1,0:T(8,128)(2,1)S(1)}, u32[]{:S(2)}, u32[]{:S(2)}) collective-permute-start(bf16[32,7168]{1,0:T(8,128)(2,1)S(1)} %collective-permute-done.4), channel_id=1, source_target_pairs={{0,1},{1,2},{2,3},{3,4},{4,5},{5,6},{6,7},{7,0},{8,9},{9,10},{10,1... | collective-permute-start | bytes 1376264 | tf_op jit(solution)/shard_map/ppermute | solution.py:27
  219.1 8.8 %collective-permute-start.6 = (bf16[32,7168]{1,0:T(8,128)(2,1)S(1)}, bf16[32,7168]{1,0:T(8,128)(2,1)S(1)}, u32[]{:S(2)}, u32[]{:S(2)}) collective-permute-start(bf16[32,7168]{1,0:T(8,128)(2,1)S(1)} %collective-permute-done.5), channel_id=1, source_target_pairs={{0,1},{1,2},{2,3},{3,4},{4,5},{5,6},{6,7},{7,0},{8,9},{9,10},{10,1... | collective-permute-start | bytes 1376264 | tf_op jit(solution)/shard_map/ppermute | solution.py:27
  228.8 11.3 %copy-start.5 = (bf16[64,512]{1,0:T(8,128)(2,1)S(1)}, bf16[64,512]{1,0:T(8,128)(2,1)}, u32[]{:S(2)}) copy-start(bf16[64,512]{1,0:T(8,128)(2,1)} %param.21) | copy-start | bytes 196612
  228.8 38.7 %copy-start.3 = (bf16[64,1024]{1,0:T(8,128)(2,1)S(1)}, bf16[64,1024]{1,0:T(8,128)(2,1)}, u32[]{:S(2)}) copy-start(bf16[64,1024]{1,0:T(8,128)(2,1)} %param.14) | copy-start | bytes 393220
  228.8 53.0 %copy-start.7 = (f32[1024]{0:T(1024)S(1)}, f32[1024]{0:T(1024)}, u32[]{:S(2)}) copy-start(f32[1024]{0:T(1024)} %param.19) | copy-start | bytes 12292
  228.8 54.8 %copy-start.8 = (f32[512]{0:T(512)S(1)}, f32[512]{0:T(512)}, u32[]{:S(2)}) copy-start(f32[512]{0:T(512)} %param.22) | copy-start | bytes 6148
  240.0 64.1 %copy-start.9 = (s32[256]{0:T(256)S(1)}, s32[256]{0:T(256)}, u32[]{:S(2)}) copy-start(s32[256]{0:T(256)} %param.25) | copy-start | bytes 3076
  240.0 64.9 %copy-start.6 = (s32[2048]{0:T(1024)S(1)}, s32[2048]{0:T(1024)}, u32[]{:S(2)}) copy-start(s32[2048]{0:T(1024)} %param.27) | copy-start | bytes 24580
  240.0 111.2 %copy-start.10 = (f32[256]{0:T(256)S(1)}, f32[256]{0:T(256)}, u32[]{:S(2)}) copy-start(f32[256]{0:T(256)} %param.24) | copy-start | bytes 3076
  240.1 64.0 %all-gather.4.cloned.1.call-start = ((), (), s32[]{:S(2)}) async-start(), calls=%async_computation.4 | async-start | bytes 1179648 | tf_op jit(solution)/shard_map/all_gather | solution.py:83
  283.5 67.7 %all-gather.8.cloned.1.call-start = ((), (), s32[]{:S(2)}) async-start(), calls=%async_computation.6 | async-start | bytes 2621440 | tf_op jit(solution)/shard_map/all_gather | solution.py:88
  294.2 138.0 %all-gather.6.cloned.1.call-start = ((), (), s32[]{:S(2)}) async-start(), calls=%async_computation.5 | async-start | bytes 5242880 | tf_op jit(solution)/shard_map/all_gather | solution.py:87
  530.8 43.8 %copy-start.1 = (s32[8,24]{1,0:T(8,128)S(1)}, s32[8,24]{1,0:T(8,128)}, u32[]{:S(2)}) copy-start(s32[8,24]{1,0:T(8,128)} %param.26) | copy-start | bytes 2308
Sparse Core Ops, SparseCore 0:
  59.4 103.6 reduce-scatter.2
  240.2 27.2 reduce-scatter.4
  283.6 20.4 all-gather.3
  305.5 45.6 all-gather.7
  352.6 79.5 all-gather.5
